TPU v7x, 256 devices: a 8x8x2 block of a 8x8x16 slice. The times are simulated.
256 devices in a mesh: grp: 2 (over z), trn: 64 (over y, x), tst: 2 (over core).
Axes of the slice: x: 8, y: 8, z: 2, core: 2. Of those that a mesh axis runs over, the one named last changes fastest.
The devices are a block of a 8x8x16 slice.
Arguments:
- test_points: bfloat16 [64, 8192], P(None, ('grp', 'tst')), parts along dimension 1, may hold values from -9 to 9
- train_points: bfloat16 [64, 524288], P(None, ('grp', 'trn')), parts along dimension 1, may hold values from -6 to 6
- weights: bfloat16 [524288], P(('grp', 'trn')), parts along dimension 0, may hold values from -6 to 6
- factor: bfloat16 [524288, 512], P(('grp', 'trn')), parts along dimension 0, may hold values from -1.14904852 to 1.14904852
Outputs:
- mean: float32 [8192], P(('grp', 'tst')), parts along dimension 0
- variance: float32 [8192], P(('grp', 'tst')), parts along dimension 0
There are 2 independent parts, one for each index of `grp`. A program takes and returns all parts, laid end to end along the dimension named above; each array names one. Nothing has to cross between parts.
All inputs are finite; a program needn't handle non-finite values.
Results may differ from a plain program's by a relative error of at most 0.0033.
Values sent between devices are 32-bit elements; how exact they have to be, the bound alone decides.
A program may use at most 64 MiB of HBM per device.

v0:
```python
import math

import jax
import jax.numpy as jnp
from jax import lax
from jax.sharding import Mesh
from jax.sharding import PartitionSpec as P

TRN = ("trn_0", "trn_1")
GRP_TRN = ("grp", "trn_0", "trn_1")


def scatter_axes(shard, axes, dim):
    if not axes:
        return shard
    nearer = lax.psum_scatter(shard, axes[0], scatter_dimension=dim, tiled=True)
    return scatter_axes(nearer, axes[1:], dim)


def turned_gather(arrays, axis, dims):
    turned = [jnp.moveaxis(a, dim, 0) for a, dim in zip(arrays, dims)]
    both = jnp.concatenate([t.reshape(len(t), -1) for t in turned], axis=1)
    result, at, outs = (lax.all_gather(both, axis, axis=0, tiled=True), 0, [])
    for t, dim in zip(turned, dims):
        piece = result[:, at : at + t[0].size].reshape(-1, *t.shape[1:])
        outs.append(jnp.moveaxis(piece, 0, dim))
        at += t[0].size
    return tuple(outs)


def on_device(test_points, train_points, weights, factor):
    rows = test_points.shape[1]
    local = train_points.shape[1]
    dim = test_points.shape[0]
    width = factor.shape[1]
    test_sq = jnp.sum(test_points.astype(jnp.float32) ** 2, axis=0)
    block = math.gcd(local, 1024)
    turns = local // block

    def step(index, carry):
        mean_acc, proj_acc = carry
        start = (index * block).astype(jnp.int32)
        points = lax.dynamic_slice_in_dim(train_points, start, block, 1)
        wblock = lax.dynamic_slice_in_dim(weights, start, block, 0)
        fblock = lax.dynamic_slice_in_dim(factor, start, block, 0)
        train_sq = jnp.sum(points.astype(jnp.float32) ** 2, axis=0)
        cross = lax.dot_general(
            test_points, points, (((0,), (0,)), ((), ())), preferred_element_type=jnp.float32
        )
        kernel = jnp.exp(
            -(test_sq[:, None] + train_sq[None, :] - 2.0 * cross) * (4.0 / dim)
        ).astype(jnp.bfloat16)
        mean_acc = mean_acc + jnp.dot(kernel, wblock, preferred_element_type=jnp.float32)
        proj_acc = proj_acc + jnp.dot(kernel, fblock, preferred_element_type=jnp.float32)
        return (mean_acc, proj_acc)

    init = (jnp.zeros((rows,), jnp.float32), jnp.zeros((rows, width), jnp.float32))
    mean_part, proj_part = lax.fori_loop(0, turns, step, init)
    mean_share, proj_share = (scatter_axes(mean_part, TRN, 0), scatter_axes(proj_part, TRN, 0))
    var_share = 1.0 - jnp.sum(proj_share * proj_share, axis=1)
    mean, variance = turned_gather((mean_share, var_share), TRN, (0, 0))
    return (mean, variance)


def solution(mesh):
    split = Mesh(
        mesh.devices.reshape(mesh.shape["grp"], 8, 8, mesh.shape["tst"]),
        ("grp", "trn_0", "trn_1", "tst"),
    )
    in_specs = (P(None, ("grp", "tst")), P(None, GRP_TRN), P(GRP_TRN), P(GRP_TRN, None))
    out_specs = (P(("grp", "tst")), P(("grp", "tst")))
    return jax.shard_map(
        on_device, mesh=split, in_specs=in_specs, out_specs=out_specs, check_vma=False
    )
```

profile of v0, /device:TPU:514, one launch (start us, length us, event | category | flops | bytes accessed | tf_op | source)
XLA Modules:
  0.0 241.4 jit_solution(6877016414136777848)
XLA Ops:
  7.2 0.1 reduce-scatter.3.cloned.1.call-start
  7.3 1.0 multiply_reduce_fusion.1
  8.3 61.1 %while.16 = (s32[]{:T(128)}, f32[2048]{0:T(1024)S(1)}, f32[2048,512]{1,0:T(8,128)}, f32[2048]{0:T(1024)S(1)}, bf16[64,4096]{1,0:T(8,128)(2,1)}, /*index=5*/bf16[...) while((s32[]{:T(128)}, f32[2048]{0:T(1024)S(1)}, ...), condition=%wide.region_3.0_spmd.clone, body=%wide.region_1.0_spmd.clone.sunk | while | flops 2434993152 | bytes 39381208 | solution.py:58
  8.3 0.9 multiply_reduce_fusion.4
  9.3 5.0 %fusion.28 = bf16[2048,1024]{0,1:T(8,128)(2,1)} fusion(bf16[64,2048]{1,0:T(8,128)(2,1)} %get-tuple-element.267, f32[1024]{0:T(1024)S(1)} %multiply_reduce_fusion.4, f32[2048]{0:T(1024)S(1)} %get-tuple-element.265, bf16[64,4096]{1,0:T(8,128)(2,1)} %get-tuple-element.266, s32[]{:T(128)S(6)} %select_n.11), kind=kOutput, calls=%fused_computation.4.clone.1 | convolution fusion | flops 281018368 | bytes 4599812 | tf_op jit(solution)/shard_map/while/body/eval_jaxpr/dot_general | solution.py:47
  14.3 0.0 copy-start
  14.3 7.0 %select_add_fusion.5 = f32[2048,512]{1,0:T(8,128)} fusion(f32[2048,512]{1,0:T(8,128)} %get-tuple-element.252, bf16[2048,1024]{0,1:T(8,128)(2,1)} %fusion.28, pred[]{:T(512)S(6)} %compare.3, bf16[4096,512]{1,0:T(8,128)(2,1)} %get-tuple-element.269, s32[]{:T(128)S(6)} %select_n.11), kind=kOutput, calls=%fused_computation.5.clone.1 | convolution fusion | flops 2149580800 | bytes 13631493 | tf_op jit(solution)/shard_map/while/body/eval_jaxpr/dot_general | solution.py:54
  21.3 0.7 dynamic_slice.36
  21.9 0.0 copy-done
  21.9 0.7 fusion.29
  22.6 0.9 multiply_reduce_fusion.4
  23.6 5.0 %fusion.28 = bf16[2048,1024]{0,1:T(8,128)(2,1)} fusion(bf16[64,2048]{1,0:T(8,128)(2,1)} %get-tuple-element.267, f32[1024]{0:T(1024)S(1)} %multiply_reduce_fusion.4, f32[2048]{0:T(1024)S(1)} %get-tuple-element.265, bf16[64,4096]{1,0:T(8,128)(2,1)} %get-tuple-element.266, s32[]{:T(128)S(6)} %select_n.11), kind=kOutput, calls=%fused_computation.4.clone.1 | convolution fusion | flops 281018368 | bytes 4599812 | tf_op jit(solution)/shard_map/while/body/eval_jaxpr/dot_general | solution.py:47
  28.6 0.0 copy-start
  28.6 8.3 %select_add_fusion.5 = f32[2048,512]{1,0:T(8,128)} fusion(f32[2048,512]{1,0:T(8,128)} %get-tuple-element.252, bf16[2048,1024]{0,1:T(8,128)(2,1)} %fusion.28, pred[]{:T(512)S(6)} %compare.3, bf16[4096,512]{1,0:T(8,128)(2,1)} %get-tuple-element.269, s32[]{:T(128)S(6)} %select_n.11), kind=kOutput, calls=%fused_computation.5.clone.1 | convolution fusion | flops 2149580800 | bytes 13631493 | tf_op jit(solution)/shard_map/while/body/eval_jaxpr/dot_general | solution.py:54
  36.8 0.7 dynamic_slice.36
  37.5 0.0 copy-done
  37.5 0.7 fusion.29
  38.2 0.9 multiply_reduce_fusion.4
  39.1 5.0 %fusion.28 = bf16[2048,1024]{0,1:T(8,128)(2,1)} fusion(bf16[64,2048]{1,0:T(8,128)(2,1)} %get-tuple-element.267, f32[1024]{0:T(1024)S(1)} %multiply_reduce_fusion.4, f32[2048]{0:T(1024)S(1)} %get-tuple-element.265, bf16[64,4096]{1,0:T(8,128)(2,1)} %get-tuple-element.266, s32[]{:T(128)S(6)} %select_n.11), kind=kOutput, calls=%fused_computation.4.clone.1 | convolution fusion | flops 281018368 | bytes 4599812 | tf_op jit(solution)/shard_map/while/body/eval_jaxpr/dot_general | solution.py:47
  44.1 0.0 copy-start
  44.1 8.3 %select_add_fusion.5 = f32[2048,512]{1,0:T(8,128)} fusion(f32[2048,512]{1,0:T(8,128)} %get-tuple-element.252, bf16[2048,1024]{0,1:T(8,128)(2,1)} %fusion.28, pred[]{:T(512)S(6)} %compare.3, bf16[4096,512]{1,0:T(8,128)(2,1)} %get-tuple-element.269, s32[]{:T(128)S(6)} %select_n.11), kind=kOutput, calls=%fused_computation.5.clone.1 | convolution fusion | flops 2149580800 | bytes 13631493 | tf_op jit(solution)/shard_map/while/body/eval_jaxpr/dot_general | solution.py:54
  52.4 0.7 dynamic_slice.36
  53.1 0.0 copy-done
  53.1 0.7 fusion.29
  53.8 0.9 multiply_reduce_fusion.4
  54.7 5.0 %fusion.28 = bf16[2048,1024]{0,1:T(8,128)(2,1)} fusion(bf16[64,2048]{1,0:T(8,128)(2,1)} %get-tuple-element.267, f32[1024]{0:T(1024)S(1)} %multiply_reduce_fusion.4, f32[2048]{0:T(1024)S(1)} %get-tuple-element.265, bf16[64,4096]{1,0:T(8,128)(2,1)} %get-tuple-element.266, s32[]{:T(128)S(6)} %select_n.11), kind=kOutput, calls=%fused_computation.4.clone.1 | convolution fusion | flops 281018368 | bytes 4599812 | tf_op jit(solution)/shard_map/while/body/eval_jaxpr/dot_general | solution.py:47
  59.7 0.0 copy-start
  59.7 8.3 %select_add_fusion.5 = f32[2048,512]{1,0:T(8,128)} fusion(f32[2048,512]{1,0:T(8,128)} %get-tuple-element.252, bf16[2048,1024]{0,1:T(8,128)(2,1)} %fusion.28, pred[]{:T(512)S(6)} %compare.3, bf16[4096,512]{1,0:T(8,128)(2,1)} %get-tuple-element.269, s32[]{:T(128)S(6)} %select_n.11), kind=kOutput, calls=%fused_computation.5.clone.1 | convolution fusion | flops 2149580800 | bytes 13631493 | tf_op jit(solution)/shard_map/while/body/eval_jaxpr/dot_general | solution.py:54
  68.0 0.7 dynamic_slice.36
  68.7 0.0 copy-done
  68.7 0.7 fusion.29
  69.3 0.0 copy-start.2
  69.4 0.0 copy-start.1
  69.4 0.1 reduce-scatter.3.cloned.1.call-update
  69.4 0.1 reduce-scatter.5.cloned.1.call-start
  69.5 74.6 %reduce-scatter.3.cloned.1.call-done = f32[256,512]{1,0:T(8,128)} async-done(((f32[2048,512]{1,0:T(8,128)}), f32[256,512]{1,0:T(8,128)}) %reduce-scatter.3.cloned.1.call-update) | async-done | bytes 524304 | tf_op jit(solution)/shard_map/reduce_scatter | solution.py:16
  144.1 0.1 reduce-scatter.5.cloned.1.call-update
  144.2 0.0 copy-done.2
  144.2 0.6 dynamic-slice
  145.4 0.0 copy-done.1
  145.4 0.6 dynamic-slice.2
  146.0 15.8 %all-reduce = f32[2048]{0:T(1024)S(1)} all-reduce(f32[2048]{0:T(1024)S(1)} %get-tuple-element.142), channel_id=2, replica_groups=mesh['grp'=2,'trn_0'=8,'trn_1'=8,'tst'=2] {'trn_0'}, use_global_device_ids=true, to_apply=%region_4.0.clone | all-reduce | flops 2048 | bytes 16384
  161.8 0.1 dynamic-slice.1
  162.5 15.7 %all-reduce.1 = f32[256]{0:T(256)S(1)} all-reduce(f32[256]{0:T(256)S(1)} %dynamic-slice.1), channel_id=3, replica_groups=mesh['grp'=2,'trn_0'=8,'trn_1'=8,'tst'=2] {'trn_1'}, use_global_device_ids=true, to_apply=%region_5.0.clone | all-reduce | flops 256 | bytes 2048
  178.2 0.1 dynamic-slice_bitcast_fusion
  178.3 5.4 %reduce-scatter.5.cloned.1.call-done = f32[32,512]{1,0:T(8,128)} async-done(((f32[256,512]{1,0:T(8,128)}), f32[32,512]{1,0:T(8,128)}) %reduce-scatter.5.cloned.1.call-update) | async-done | bytes 65552 | tf_op jit(solution)/shard_map/reduce_scatter | solution.py:16
  183.7 1.0 multiply_reduce_fusion.2
  184.7 49.1 %all-gather = f32[64,32,2]{1,2,0:T(2,128)S(1)} all-gather(f32[1,32,2]{1,2,0:T(2,128)S(1)} %maximum_bitcast_fusion), channel_id=1, replica_groups=mesh['grp'=2,'trn_0'=8,'trn_1'=8,'tst'=2] {'trn_0','trn_1'}, dimensions={0}, use_global_device_ids=true | all-gather | bytes 16640 | tf_op jit(solution)/shard_map/all_gather | solution.py:23
  233.8 0.1 reshape.29
  233.9 0.6 fusion.8
  (13 shorter events, 0.1 us)
Async XLA Ops:
  7.2 136.9 %reduce-scatter.3.cloned.1.call-start = ((), (), s32[]{:S(2)}) async-start(), calls=%async_computation.2 | async-start | bytes 4718592 | tf_op jit(solution)/shard_map/reduce_scatter | solution.py:16
  14.3 7.7 %copy-start = (bf16[2048,1024]{0,1:T(8,128)(2,1)S(1)}, bf16[2048,1024]{0,1:T(8,128)(2,1)}, u32[]{:S(2)}) copy-start(bf16[2048,1024]{0,1:T(8,128)(2,1)} %fusion.28) | copy-start | bytes 12582916 | tf_op jit(solution)/shard_map/while
  28.6 9.0 %copy-start = (bf16[2048,1024]{0,1:T(8,128)(2,1)S(1)}, bf16[2048,1024]{0,1:T(8,128)(2,1)}, u32[]{:S(2)}) copy-start(bf16[2048,1024]{0,1:T(8,128)(2,1)} %fusion.28) | copy-start | bytes 12582916 | tf_op jit(solution)/shard_map/while
  44.1 9.0 %copy-start = (bf16[2048,1024]{0,1:T(8,128)(2,1)S(1)}, bf16[2048,1024]{0,1:T(8,128)(2,1)}, u32[]{:S(2)}) copy-start(bf16[2048,1024]{0,1:T(8,128)(2,1)} %fusion.28) | copy-start | bytes 12582916 | tf_op jit(solution)/shard_map/while
  59.7 9.0 %copy-start = (bf16[2048,1024]{0,1:T(8,128)(2,1)S(1)}, bf16[2048,1024]{0,1:T(8,128)(2,1)}, u32[]{:S(2)}) copy-start(bf16[2048,1024]{0,1:T(8,128)(2,1)} %fusion.28) | copy-start | bytes 12582916 | tf_op jit(solution)/shard_map/while
  69.3 74.8 %copy-start.2 = (u32[256]{0:T(256)S(1)}, u32[256]{0:T(256)}, u32[]{:S(2)}) copy-start(u32[256]{0:T(256)} %constant.56) | copy-start | bytes 3076
  69.4 76.1 %copy-start.1 = (u32[256]{0:T(256)S(1)}, u32[256]{0:T(256)}, u32[]{:S(2)}) copy-start(u32[256]{0:T(256)} %constant.60) | copy-start | bytes 3076
  69.4 114.3 %reduce-scatter.5.cloned.1.call-start = ((), (), s32[]{:S(2)}) async-start(), calls=%async_computation.3 | async-start | bytes 589824 | tf_op jit(solution)/shard_map/reduce_scatter | solution.py:16
Sparse Core Ops, SparseCore 0:
  69.5 74.5 reduce-scatter.2
  146.7 37.0 reduce-scatter.4
where the time goes:
time: 242 us; the launch traced here: 241 us
  blocking collectives  80.6 us (33%)
  waiting for transfers between devices  80.1 us (33%)
  matrix products  54.4 us (22%)
  between operations  15.4 us (6%)
  other arithmetic  5.82 us (2%)
  local copies, waits for them, and re-layouts  4.83 us (2%)
    reduce_scatter x2, waiting for transfers between devices, scatter_axes(): nearer = lax.psum_scatter(shard, axes[0], scatter_dimension=dim, tiled=True)  80 us
    all_gather x1, blocking collectives, turned_gather(): result, at, outs = (lax.all_gather(both, axis, axis=0, tiled=True), 0, [])  49.1 us
    dot_general x4, matrix products, step(): jnp.dot(kernel, fblock, preferred_element_type=jnp.float32)  31.8 us
    unnamed x2, blocking collectives  31.5 us
    dot_general x4, matrix products, step(): lax.dot_general(test_points, points, (((0,), (0,)), ((), ())), preferred_...  20 us
  transfers between devices with their start and end apart: 2, of which 2 were waited for; matrix products, arithmetic and copies ran while one was open for 1% of the time, Pallas kernels for 0%

commit v1 on v0

v1 whole, which is shorter than its diff:
```python
import functools
import math

import jax
import jax.numpy as jnp
from jax import lax
from jax.experimental import pallas as pl
from jax.experimental.pallas import tpu as pltpu
from jax.sharding import PartitionSpec as P

LOG2E = 1.4426950408889634
F32 = jnp.float32
BF16 = jnp.bfloat16
LANES = 128


def pieces_of(value):
    hi = value.astype(BF16).astype(F32)
    rest = value - hi
    mid = rest.astype(BF16).astype(F32)
    low = (rest - mid).astype(BF16).astype(F32)
    return hi, mid, low


def norm_rows(pieces, ones_first, width):
    row = lax.broadcasted_iota(jnp.int32, (16, width), 0)
    base = 3 if ones_first else 0
    ones = 0 if ones_first else 3
    block = jnp.where((row >= ones) & (row < ones + 3), F32(1), F32(0))
    for k, piece in enumerate(pieces):
        block = jnp.where(row == base + k, jnp.broadcast_to(piece, (16, width)), block)
    return block


def body(
    side, chunk,
    test_ref, train_ref, weight_ref, factor_hbm, mean_ref, var_ref,
    factor, lhs, rhs, send_r, send_l, recv_r, recv_l, part, msg, gather,
    load_sem, sr_sem, sl_sem, rr_sem, rl_sem, ps_sem, pr_sem, gs_sem, gr_sem,
):
    dim = test_ref.shape[0]
    local = train_ref.shape[1]
    rank = factor.shape[1]
    half = side // 2
    slots = side - 1
    me = lax.axis_index("trn")
    tst = lax.axis_index("tst")
    row_pos, col_pos = lax.div(me, side), lax.rem(me, side)
    pos1 = jnp.where(tst == 0, col_pos, row_pos)
    pos2 = jnp.where(tst == 0, row_pos, col_pos)
    stride1 = jnp.where(tst == 0, 1, side)
    stride2 = jnp.where(tst == 0, side, 1)

    def at(p1, p2):
        return p1 * stride1 + p2 * stride2

    right = at(lax.rem(pos1 + 1, side), pos2)
    left = at(lax.rem(pos1 + side - 1, side), pos2)

    step_rows = local // 4
    loads = []
    for c in range(4):
        rows = pl.ds(c * step_rows, step_rows)
        copy = pltpu.make_async_copy(factor_hbm.at[rows], factor.at[rows], load_sem.at[c])
        copy.start()
        loads.append(copy)
    barrier = pltpu.get_barrier_semaphore()
    for peer in (right, left):
        pl.semaphore_signal(barrier, inc=1, device_id={"trn": peer})
    for k in range(1, side):
        pl.semaphore_signal(barrier, inc=1, device_id={"trn": at(pos1, lax.rem(pos2 + k, side))})

    scale = 4.0 / dim
    train = train_ref[...].astype(F32)
    tsq = jnp.sum(train * train, axis=0, keepdims=True) * F32(-scale * LOG2E)
    parts = pieces_of(train * F32(2.0 * scale * LOG2E))
    for k in range(3):
        rhs[k * dim : (k + 1) * dim, :] = parts[k].astype(BF16)
    rhs[3 * dim : 3 * dim + 16, :] = norm_rows(pieces_of(tsq), False, local).astype(BF16)
    rhs[3 * dim + 16 :, :] = jnp.zeros((rhs.shape[0] - 3 * dim - 16, local), BF16)

    wide = 2 * LANES

    def turn(b, carry):
        cols = pl.ds(pl.multiple_of(b * wide, wide), wide)
        test = test_ref[:, cols].astype(F32)
        ssq = jnp.sum(test * test, axis=0, keepdims=True) * F32(-scale * LOG2E)
        rows = norm_rows(pieces_of(ssq), True, wide)
        pad = jnp.zeros((lhs.shape[1] - 3 * dim - 16, wide), F32)
        stack = jnp.concatenate([test, test, test, rows, pad], axis=0)
        lhs[cols, :] = stack.T.astype(BF16)
        return carry

    lax.fori_loop(0, test_ref.shape[1] // wide, turn, 0)
    for copy in loads:
        copy.wait()
    pl.semaphore_wait(barrier, 2 + side - 1)

    def copies(s):
        to_right = pltpu.make_async_remote_copy(
            src_ref=send_r.at[s], dst_ref=recv_r.at[s],
            send_sem=sr_sem.at[s], recv_sem=rr_sem.at[s], device_id={"trn": right},
        )
        to_left = pltpu.make_async_remote_copy(
            src_ref=send_l.at[s], dst_ref=recv_l.at[s],
            send_sem=sl_sem.at[s], recv_sem=rl_sem.at[s], device_id={"trn": left},
        )
        return to_right, to_left

    def slot(s, carry):
        distance = lax.div(side - s, 2)
        odd = lax.rem(s, 2)
        block_r = lax.rem(pos1 + distance, side)
        block_l = lax.rem(pos1 + side - distance, side)
        start_r = pl.multiple_of((block_r * 2 + odd) * LANES, LANES)
        start_l = pl.multiple_of((block_l * 2 + 1 - odd) * LANES, LANES)
        points = jnp.concatenate([lhs[pl.ds(start_r, LANES), :], lhs[pl.ds(start_l, LANES), :]], axis=0)
        total = jnp.zeros((wide, rank), F32)
        weighted = jnp.zeros((wide, LANES), F32)
        for c in range(local // chunk):
            cols = slice(c * chunk, (c + 1) * chunk)
            power = jnp.dot(points, rhs[:, cols], preferred_element_type=F32)
            kern = jnp.exp2(power).astype(BF16)
            total = total + jnp.dot(kern, factor[cols, :], preferred_element_type=F32)
            terms = kern.astype(F32) * weight_ref[:, cols].astype(F32)
            for g in range(chunk // LANES):
                weighted = weighted + terms[:, g * LANES : (g + 1) * LANES]
        for k, ref in enumerate((send_r, send_l)):
            rows = slice(k * LANES, (k + 1) * LANES)
            ref[s, :rank, :] = total[rows].T
            mean_row = jnp.sum(weighted[rows].T, axis=0, keepdims=True)
            ref[s, rank:, :] = jnp.broadcast_to(mean_row, (8, LANES))

        @pl.when(s >= 2)
        def _():
            to_right, to_left = copies(s - 2)
            to_right.wait_recv()
            to_left.wait_recv()
            send_r[s] = send_r[s] + recv_r[s - 2]
            send_l[s] = send_l[s] + recv_l[s - 2]

        @pl.when(s < slots)
        def _():
            to_right, to_left = copies(s)
            to_right.start()
            to_left.start()

        return carry

    lax.fori_loop(0, side, slot, 0)
    last_r, last_l = copies(slots - 1)
    last_r.wait_recv()
    last_l.wait_recv()
    send_l[slots] = send_l[slots] + recv_r[slots - 1]
    send_r[slots] = send_r[slots] + recv_l[slots - 1]

    share = rank // side
    sums = (send_l, send_r)

    def exchange(k, h):
        peer = lax.rem(pos2 + k, side)
        rows = pl.ds(pl.multiple_of(peer * share, share), share)
        return pltpu.make_async_remote_copy(
            src_ref=sums[h].at[slots, rows], dst_ref=part.at[k - 1, h],
            send_sem=ps_sem.at[k - 1, h], recv_sem=pr_sem.at[k - 1, h],
            device_id={"trn": at(pos1, peer)},
        )

    for k in range(1, side):
        for h in range(2):
            exchange(k, h).start()
    mine = pl.ds(pl.multiple_of(pos2 * share, share), share)
    squares = []
    for h in range(2):
        block = sums[h][slots, mine, :]
        for k in range(1, side):
            exchange(k, h).wait_recv()
            block = block + part[k - 1, h]
        squares.append(jnp.sum(block * block, axis=0, keepdims=True))
    line = lax.broadcasted_iota(jnp.int32, (4, LANES), 0)
    values = squares + [send_l[slots, rank : rank + 1, :], send_r[slots, rank : rank + 1, :]]
    packed = jnp.zeros((4, LANES), F32)
    for k, value in enumerate(values):
        packed = jnp.where(line == k, jnp.broadcast_to(value, (4, LANES)), packed)
    msg[...] = packed

    own = pos1 * side + pos2

    def spread(k):
        other = lax.rem(own + k, side * side)
        return pltpu.make_async_remote_copy(
            src_ref=msg, dst_ref=gather.at[own], send_sem=gs_sem, recv_sem=gr_sem,
            device_id={"trn": at(lax.div(other, side), lax.rem(other, side))},
        )

    def send(k, carry):
        spread(k).start()
        return carry

    lax.fori_loop(1, side * side, send, 0)
    gather[own] = packed

    def drain(s, carry):
        to_right, to_left = copies(s)
        to_right.wait_send()
        to_left.wait_send()
        return carry

    lax.fori_loop(0, slots, drain, 0)
    for k in range(1, side):
        for h in range(2):
            exchange(k, h).wait_send()
    others = gather.at[pl.ds(0, side * side - 1)]
    pltpu.make_async_remote_copy(
        src_ref=others, dst_ref=others, send_sem=gs_sem, recv_sem=gr_sem, device_id={"trn": right}
    ).wait()
    for p in range(side):
        total = gather[p * side]
        for q in range(1, side):
            total = total + gather[p * side + q]
        var_ref[p] = 1.0 - total[0:2]
        mean_ref[p] = total[2:4]


def on_device(side, test_points, train_points, weights, factor):
    dim, rows = test_points.shape
    local, rank = factor.shape
    slots = side - 1
    depth = 2 * LANES
    share = rank // side
    dma = pltpu.SemaphoreType.DMA
    vmem = pl.BlockSpec(memory_space=pltpu.VMEM)
    chunk_shape = (rank + 8, LANES)
    mean, var = pl.pallas_call(
        functools.partial(body, side, 1024),
        out_shape=[jax.ShapeDtypeStruct((side, 2, LANES), F32)] * 2,
        in_specs=[vmem, vmem, vmem, pl.BlockSpec(memory_space=pl.ANY)],
        out_specs=[vmem, vmem],
        scratch_shapes=[
            pltpu.VMEM((local, rank), BF16),
            pltpu.VMEM((rows, depth), BF16),
            pltpu.VMEM((depth, local), BF16),
            pltpu.VMEM((side, *chunk_shape), F32),
            pltpu.VMEM((side, *chunk_shape), F32),
            pltpu.VMEM((slots, *chunk_shape), F32),
            pltpu.VMEM((slots, *chunk_shape), F32),
            pltpu.VMEM((slots, 2, share, LANES), F32),
            pltpu.VMEM((4, LANES), F32),
            pltpu.VMEM((side * side, 4, LANES), F32),
            dma((4,)),
            dma((slots,)), dma((slots,)), dma((slots,)), dma((slots,)),
            dma((slots, 2)), dma((slots, 2)),
            dma, dma,
        ],
        compiler_params=pltpu.CompilerParams(
            collective_id=0, has_side_effects=True, vmem_limit_bytes=56 * 1024 * 1024
        ),
    )(test_points, train_points, weights.reshape(1, local), factor)
    return mean.reshape(rows), var.reshape(rows)


def solution(mesh):
    side = math.isqrt(mesh.shape["trn"])
    shared = ("grp", "trn")
    return jax.shard_map(
        functools.partial(on_device, side),
        mesh=mesh,
        in_specs=(P(None, ("grp", "tst")), P(None, shared), P(shared), P(shared, None)),
        out_specs=(P(("grp", "tst")), P(("grp", "tst"))),
        check_vma=False,
    )
```

time: 242 us -> 77 us (0.32)
  blocking collectives: 80.6 us -> 0 us
  waiting for transfers between devices: 80.1 us -> 0 us
  Pallas kernels: 0 us -> 72.2 us
  matrix products: 54.4 us -> 0 us
  between operations: 15.4 us -> 0.64 us
  other arithmetic: 5.82 us -> 0 us
    reduce_scatter x2 -> x0, waiting for transfers between devices: 80 us -> none  [scatter_axes(): nearer = lax.psum_scatter(shard, axes[0], scatter_dimension=dim, tiled=True)]
    pallas_call x0 -> x1, Pallas kernels: none -> 72.2 us  [on_device(): pl.pallas_call(functools.partial(body, side, 1024), out_shape=[jax.ShapeD...]
    dot_general x12 -> x0, matrix products: 54.4 us -> none  [the longest x4 31.8 us: step(): jnp.dot(kernel, fblock, preferred_element_type=jnp.float32)]
    all_gather x1 -> x0, blocking collectives: 49.1 us -> none  [turned_gather(): result, at, outs = (lax.all_gather(both, axis, axis=0, tiled=True), 0, [])]
    unnamed x2 -> x0, blocking collectives: 31.5 us -> none
    reduce_sum x6 -> x0, other arithmetic: 5.77 us -> none  [the longest x4 3.79 us: step(): train_sq = jnp.sum(points.astype(jnp.float32) ** 2, axis=0)]
    dynamic_slice x8 -> x0, local copies, waits for them, and re-layouts: 2.76 us -> none  [step(): wblock = lax.dynamic_slice_in_dim(weights, start, block, 0)]
  transfers between devices with their start and end apart: 2 -> 0, of which waited for: 2 -> 0; matrix products, arithmetic and copies ran while one was open for 1% -> 0% of each run, Pallas kernels for 0% -> 0%
where the time goes in v1:
time: 77 us; the launch traced here: 76.7 us
  Pallas kernels  72.2 us (94%)
  local copies, waits for them, and re-layouts  3.9 us (5%)
    pallas_call x1, Pallas kernels, on_device(): pl.pallas_call(functools.partial(body, side, 1024), out_shape=[jax.ShapeD...  72.2 us
    unnamed x2, local copies, waits for them, and re-layouts  2.59 us

profile of v1, /device:TPU:514, one launch (start us, length us, event | category | flops | bytes accessed | tf_op | source)
XLA Modules:
  0.0 76.7 jit_solution(9408523548541707042)
XLA Ops:
  0.6 1.3 %reshape.13.weight_ref = bf16[1,4096]{1,0:T(2,128)(2,1)} reshape(bf16[4096]{0:T(1024)(128)(2,1)} %param.6) | data formatting | bytes 16384 | tf_op jit(solution)/shard_map/reshape | solution.py:258
  1.9 72.2 %shard_map.59 = (f32[8,2,128]{2,1,0:T(2,128)}, f32[8,2,128]{2,1,0:T(2,128)}) custom-call(bf16[64,2048]{1,0:T(8,128)(2,1)} %test_ref.1, bf16[64,4096]{1,0:T(8,128)(2,1)} %train_ref.1, bf16[1,4096]{1,0:T(2,128)(2,1)} %reshape.13.weight_ref, bf16[4096,512]{1,0:T(8,128)(2,1)} %factor_hbm.1), custom_call_target="tpu_custom_call" | custom-call | tf_op jit(solution)/shard_map/pallas_call | solution.py:234
  74.1 1.3 %copy.8 = f32[2048]{0:T(1024)} copy(f32[2048]{0:T(1024)} %bitcast.3) | data formatting | bytes 16384
  75.4 1.3 %copy.9 = f32[2048]{0:T(1024)} copy(f32[2048]{0:T(1024)} %bitcast.2) | data formatting | bytes 16384

commit v2 on v1

v2 whole, which is shorter than its diff:
```python
import functools
import math

import jax
import jax.numpy as jnp
from jax import lax
from jax.experimental import pallas as pl
from jax.experimental.pallas import tpu as pltpu
from jax.sharding import PartitionSpec as P

LOG2E = 1.4426950408889634
F32 = jnp.float32
BF16 = jnp.bfloat16
LANES = 128


def pieces_of(value):
    hi = value.astype(BF16).astype(F32)
    rest = value - hi
    mid = rest.astype(BF16).astype(F32)
    low = (rest - mid).astype(BF16).astype(F32)
    return hi, mid, low


def norm_rows(pieces, ones_first, width):
    row = lax.broadcasted_iota(jnp.int32, (16, width), 0)
    base = 3 if ones_first else 0
    ones = 0 if ones_first else 3
    block = jnp.where((row >= ones) & (row < ones + 3), F32(1), F32(0))
    for k, piece in enumerate(pieces):
        block = jnp.where(row == base + k, jnp.broadcast_to(piece, (16, width)), block)
    return block


def body(
    side, chunk,
    test_ref, train_ref, weight_ref, factor_hbm, out_ref,
    factor, lhs, rhs, part, recv, share_in, msg, gather,
    load_sem, s_sem, r_sem, ps_sem, pr_sem, gs_sem, gr_sem,
):
    dim = test_ref.shape[0]
    local = train_ref.shape[1]
    rank = factor.shape[1]
    half = side // 2
    slots = side - 1
    wide = 2 * LANES
    me = lax.axis_index("trn")
    row_pos, col_pos = lax.div(me, side), lax.rem(me, side)
    pos = (col_pos, row_pos)
    stride = (1, side)

    def moved(axis, k):
        there = lax.rem(pos[axis] + k + side, side)
        return me + (there - pos[axis]) * stride[axis]

    step_rows = local // 4
    loads = []
    for c in range(4):
        rows = pl.ds(c * step_rows, step_rows)
        copy = pltpu.make_async_copy(factor_hbm.at[rows], factor.at[rows], load_sem.at[c])
        copy.start()
        loads.append(copy)
    barrier = pltpu.get_barrier_semaphore()
    for axis in range(2):
        for k in range(1, side):
            pl.semaphore_signal(barrier, inc=1, device_id={"trn": moved(axis, k)})

    scale = 4.0 / dim
    train = train_ref[...].astype(F32)
    tsq = jnp.sum(train * train, axis=0, keepdims=True) * F32(-scale * LOG2E)
    parts = pieces_of(train * F32(2.0 * scale * LOG2E))
    for k in range(3):
        rhs[k * dim : (k + 1) * dim, :] = parts[k].astype(BF16)
    rhs[3 * dim : 3 * dim + 16, :] = norm_rows(pieces_of(tsq), False, local).astype(BF16)
    rhs[3 * dim + 16 :, :] = jnp.zeros((rhs.shape[0] - 3 * dim - 16, local), BF16)

    def turn(b, carry):
        cols = pl.ds(pl.multiple_of(b * wide, wide), wide)
        test = test_ref[:, cols].astype(F32)
        ssq = jnp.sum(test * test, axis=0, keepdims=True) * F32(-scale * LOG2E)
        rows = norm_rows(pieces_of(ssq), True, wide)
        pad = jnp.zeros((lhs.shape[1] - 3 * dim - 16, wide), F32)
        stack = jnp.concatenate([test, test, test, rows, pad], axis=0)
        lhs[cols, :] = stack.T.astype(BF16)
        return carry

    lax.fori_loop(0, test_ref.shape[1] // wide, turn, 0)
    for copy in loads:
        copy.wait()

    cut = rank // 2
    halves = (pl.ds(0, cut), pl.ds(cut, rank + 8 - cut))

    def place(way, distance):
        return distance if way == 0 or distance in (0, half) else half + distance

    def piece(way, s):
        return halves[(s + way) % 2]

    def hop(axis, way, s):
        rows = piece(way, s)
        return pltpu.make_async_remote_copy(
            src_ref=part.at[axis, place(way, (side - s) // 2), rows],
            dst_ref=recv.at[axis, way, s, pl.ds(0, rows.size)],
            send_sem=s_sem.at[axis, way, s], recv_sem=r_sem.at[axis, way, s],
            device_id={"trn": moved(axis, 1 if way == 0 else -1)},
        )

    def take(axis, way, s, distance):
        hop(axis, way, s).wait_recv()
        rows = piece(way, s)
        at = place(way, distance)
        part[axis, at, rows, :] = part[axis, at, rows, :] + recv[axis, way, s, : rows.size, :]

    def send(axis, s):
        for way in range(2):
            if s >= 2:
                take(axis, way, s - 2, (side - s) // 2)
            hop(axis, way, s).start()

    plan = {
        0: [(0, 0), (1, 0)],
        1: [(0, 1)],
        2: [(1, 1)],
        3: [(0, 2), (1, 2)],
        5: [(0, 3), (1, 3)],
        6: [(0, 4), (1, 4)],
        7: [(0, 5), (1, 5), (0, 6), (1, 6)],
    }

    def compute(i, carry):
        edge = (i == 0) | (i == side - 1)
        inner = lax.rem(i + 1, 2)
        distance = half - lax.div(i + 1, 2)
        distance = jnp.where(i == 0, half, jnp.where(i == side - 1, 0, distance))
        axes = (jnp.where(edge, 0, inner), jnp.where(edge, 1, inner))
        signed = (distance, jnp.where(edge, distance, -distance))
        places = (distance, jnp.where(edge, distance, half + distance))
        starts = []
        for k in range(2):
            at = jnp.where(axes[k] == 0, col_pos, row_pos)
            block = lax.rem(at + signed[k] + side, side)
            starts.append(pl.multiple_of((block * 2 + axes[k]) * LANES, LANES))
        points = jnp.concatenate([lhs[pl.ds(s, LANES), :] for s in starts], axis=0)
        total = jnp.zeros((wide, rank), F32)
        weighted = jnp.zeros((wide, LANES), F32)
        for c in range(local // chunk):
            cols = slice(c * chunk, (c + 1) * chunk)
            power = jnp.dot(points, rhs[:, cols], preferred_element_type=F32)
            kern = jnp.exp2(power).astype(BF16)
            total = total + jnp.dot(kern, factor[cols, :], preferred_element_type=F32)
            terms = kern.astype(F32) * weight_ref[cols].reshape(1, chunk).astype(F32)
            for g in range(chunk // LANES):
                weighted = weighted + terms[:, g * LANES : (g + 1) * LANES]
        for k in range(2):
            rows = slice(k * LANES, (k + 1) * LANES)
            part[axes[k], places[k], :rank, :] = total[rows].T
            mean_row = jnp.sum(weighted[rows].T, axis=0, keepdims=True)
            part[axes[k], places[k], rank:, :] = jnp.broadcast_to(mean_row, (8, LANES))

        for when, sends in plan.items():
            @pl.when(i == when)
            def _(when=when, sends=sends):
                if when == 0:
                    pl.semaphore_wait(barrier, 2 * slots)
                for axis, s in sends:
                    send(axis, s)

        return carry

    lax.fori_loop(0, side, compute, 0)

    share = rank // side
    order = sorted(range(1, side), key=lambda k: -min(k, side - k))

    def exchange(axis, k):
        peer = lax.rem(pos[1 - axis] + k, side)
        rows = pl.ds(pl.multiple_of(peer * share, share), share)
        return pltpu.make_async_remote_copy(
            src_ref=part.at[axis, 0, rows], dst_ref=share_in.at[axis, k - 1],
            send_sem=ps_sem.at[axis, k - 1], recv_sem=pr_sem.at[axis, k - 1],
            device_id={"trn": moved(1 - axis, k)},
        )

    for axis in range(2):
        for s in (slots - 2, slots - 1):
            for way in range(2):
                take(axis, way, s, 0)
        for k in order:
            exchange(axis, k).start()
    values = []
    for axis in range(2):
        mine = pl.ds(pl.multiple_of(pos[1 - axis] * share, share), share)
        block = part[axis, 0, mine, :]
        for k in range(1, side):
            exchange(axis, k).wait_recv()
            block = block + share_in[axis, k - 1]
        values.append(jnp.sum(block * block, axis=0, keepdims=True))
        values.append(part[axis, 0, rank : rank + 1, :])
    line = lax.broadcasted_iota(jnp.int32, (4, LANES), 0)
    packed = jnp.zeros((4, LANES), F32)
    for k, value in enumerate(values):
        packed = jnp.where(line == k, jnp.broadcast_to(value, (4, LANES)), packed)
    msg[...] = packed

    count = side * side

    def spread(j):
        k = lax.rem(j + count // 2 + half, count - 1) + 1
        other = lax.rem(me + k, count)
        return pltpu.make_async_remote_copy(
            src_ref=msg, dst_ref=gather.at[me], send_sem=gs_sem, recv_sem=gr_sem, device_id={"trn": other}
        )

    def tell(j, carry):
        spread(j).start()
        return carry

    lax.fori_loop(0, count - 1, tell, 0)
    gather[me] = packed
    for axis in range(2):
        for way in range(2):
            for s in range(slots):
                hop(axis, way, s).wait_send()
        for k in order:
            exchange(axis, k).wait_send()
    others = gather.at[pl.ds(0, count - 1)]
    pltpu.make_async_remote_copy(
        src_ref=others, dst_ref=others, send_sem=gs_sem, recv_sem=gr_sem, device_id={"trn": moved(0, 1)}
    ).wait()
    for p in range(side):
        for axis in range(2):
            total = jnp.zeros((4, LANES), F32)
            for q in range(side):
                total = total + gather[q * side + p if axis == 0 else p * side + q]
            row = 2 * p + axis
            out_ref[0, row : row + 1, :] = total[2 * axis : 2 * axis + 1]
            out_ref[1, row : row + 1, :] = -total[2 * axis + 1 : 2 * axis + 2]


def on_device(side, test_points, train_points, weights, factor):
    dim, rows = test_points.shape
    local, rank = factor.shape
    slots = side - 1
    depth = 2 * LANES
    share = rank // side
    dma = pltpu.SemaphoreType.DMA
    vmem = pl.BlockSpec(memory_space=pltpu.VMEM)
    out = pl.pallas_call(
        functools.partial(body, side, 1024),
        out_shape=jax.ShapeDtypeStruct((2, rows // LANES, LANES), F32),
        in_specs=[vmem, vmem, vmem, pl.BlockSpec(memory_space=pl.ANY)],
        out_specs=vmem,
        scratch_shapes=[
            pltpu.VMEM((local, rank), BF16),
            pltpu.VMEM((rows, depth), BF16),
            pltpu.VMEM((depth, local), BF16),
            pltpu.VMEM((2, side, rank + 8, LANES), F32),
            pltpu.VMEM((2, 2, slots, rank // 2 + 8, LANES), F32),
            pltpu.VMEM((2, slots, share, LANES), F32),
            pltpu.VMEM((4, LANES), F32),
            pltpu.VMEM((side * side, 4, LANES), F32),
            dma((4,)),
            dma((2, 2, slots)), dma((2, 2, slots)),
            dma((2, slots)), dma((2, slots)),
            dma, dma,
        ],
        compiler_params=pltpu.CompilerParams(
            collective_id=0, has_side_effects=True, vmem_limit_bytes=56 * 1024 * 1024
        ),
    )(test_points, train_points, weights, factor)
    return -out[1].reshape(rows), 1.0 - out[0].reshape(rows)


def solution(mesh):
    side = math.isqrt(mesh.shape["trn"])
    shared = ("grp", "trn")
    return jax.shard_map(
        functools.partial(on_device, side),
        mesh=mesh,
        in_specs=(P(None, ("grp", "tst")), P(None, shared), P(shared), P(shared, None)),
        out_specs=(P(("grp", "tst")), P(("grp", "tst"))),
        check_vma=False,
    )
```

time: 77 us -> 64.9 us (0.84)
  Pallas kernels: 72.2 us -> 62.7 us
  local copies, waits for them, and re-layouts: 3.9 us -> 0 us
  other arithmetic: 0 us -> 1.32 us
    pallas_call x1, Pallas kernels: 72.2 us -> 62.7 us  [on_device(): pl.pallas_call(functools.partial(body, side, 1024), out_shape=jax.ShapeDt...]
    unnamed x2 -> x0, local copies, waits for them, and re-layouts: 2.59 us -> none
    sub x0 -> x1, other arithmetic: none -> 1.32 us  [on_device(): return (-out[1].reshape(rows), 1.0 - out[0].reshape(rows))]
    reshape x1 -> x0, local copies, waits for them, and re-layouts: 1.31 us -> none  [on_device(): weights.reshape(1, local)]
where the time goes in v2:
time: 64.9 us; the launch traced here: 64.7 us
  Pallas kernels  62.7 us (97%)
  other arithmetic  1.32 us (2%)
    pallas_call x1, Pallas kernels, on_device(): pl.pallas_call(functools.partial(body, side, 1024), out_shape=jax.ShapeDt...  62.7 us
    sub x1, other arithmetic, on_device(): return (-out[1].reshape(rows), 1.0 - out[0].reshape(rows))  1.32 us

profile of v2, /device:TPU:514, one launch (start us, length us, event | category | flops | bytes accessed | tf_op | source)
XLA Modules:
  0.0 64.7 jit_solution(7753387996236886852)
XLA Ops:
  0.6 62.7 %shard_map.59 = f32[2,16,128]{2,1,0:T(8,128)} custom-call(bf16[64,2048]{1,0:T(8,128)(2,1)} %test_ref.1, bf16[64,4096]{1,0:T(8,128)(2,1)} %train_ref.1, bf16[4096]{0:T(1024)(128)(2,1)} %weight_ref.1, bf16[4096,512]{1,0:T(8,128)(2,1)} %factor_hbm.1), custom_call_target="tpu_custom_call" | custom-call | tf_op jit(solution)/shard_map/pallas_call | solution.py:249
  63.4 1.3 %subtract_bitcast_fusion = (f32[2048]{0:T(1024)}, f32[2048]{0:T(1024)}) fusion(f32[2,16,128]{2,1,0:T(8,128)} %shard_map.59), kind=kLoop, calls=%fused_computation | loop fusion | flops 4096 | bytes 32768 | tf_op jit(solution)/shard_map/sub | solution.py:272

commit v3 on v2

v3 whole, which is shorter than its diff:
```python
import functools
import math

import jax
import jax.numpy as jnp
from jax import lax
from jax.experimental import pallas as pl
from jax.experimental.pallas import tpu as pltpu
from jax.sharding import PartitionSpec as P

LOG2E = 1.4426950408889634
F32 = jnp.float32
BF16 = jnp.bfloat16
LANES = 128


def pieces_of(value):
    hi = value.astype(BF16).astype(F32)
    rest = value - hi
    mid = rest.astype(BF16).astype(F32)
    low = (rest - mid).astype(BF16).astype(F32)
    return hi, mid, low


def norm_rows(values, ones_first):
    width = values.shape[1]
    row = lax.broadcasted_iota(jnp.int32, (16, width), 0)
    base, ones = (3, 0) if ones_first else (0, 3)
    block = jnp.where((row >= ones) & (row < ones + 3), F32(1), F32(0))
    for k, piece in enumerate(pieces_of(values)):
        block = jnp.where(row == base + k, jnp.broadcast_to(piece, (16, width)), block)
    return block


def half_norms(points):
    points = points.astype(F32)
    return jnp.sum(points * points, axis=0, keepdims=True) * F32(-0.5)


def body(
    side, chunk,
    test_hbm, train_hbm, weight_hbm, factor_hbm, out_ref,
    test, train, weight, factor, lhs, rhs, part, recv, share_in, mean_own, mean_in, mean_all, msg, gather,
    load_sem, s_sem, r_sem, ps_sem, pr_sem, ms_sem, mr_sem, gs_sem, gr_sem, as_sem, ar_sem,
):
    dim, local = train.shape
    rank = factor.shape[1]
    half = side // 2
    slots = side - 1
    wide = 2 * LANES
    turns = local // chunk
    me = lax.axis_index("trn")
    row_pos, col_pos = lax.div(me, side), lax.rem(me, side)
    pos = (col_pos, row_pos)
    ring = [
        [lax.rem(pos[axis] + k, side) * (1, side)[axis] for k in range(side)] for axis in range(2)
    ]

    def moved(axis, k):
        k = k % side
        return ring[0][k] + ring[1][0] if axis == 0 else ring[0][0] + ring[1][k]

    def load(k, src, dst):
        copy = pltpu.make_async_copy(src, dst, load_sem.at[k])
        copy.start()
        return copy

    get_test = load(0, test_hbm, test)
    get_train = load(1, train_hbm, train)
    get_weight = load(2, weight_hbm, weight)
    get_factor = []
    for c in range(turns):
        rows = pl.ds(c * chunk, chunk)
        get_factor.append(load(3 + c, factor_hbm.at[rows], factor.at[rows]))
    barrier = pltpu.get_barrier_semaphore()
    for axis in range(2):
        for k in range(1, side):
            pl.semaphore_signal(barrier, inc=1, device_id={"trn": moved(axis, k)})

    pad = jnp.zeros((LANES - dim - 16, LANES), F32)
    get_test.wait()
    for b in range(test.shape[1] // LANES):
        cols = slice(b * LANES, (b + 1) * LANES)
        points = test[:, cols].astype(F32)
        stack = jnp.concatenate([points, norm_rows(half_norms(points), True), pad], axis=0)
        lhs[cols, :] = stack.T.astype(BF16)
    get_train.wait()
    rhs[dim + 16 :, :] = jnp.zeros((LANES - dim - 16, local), BF16)
    for c in range(turns):
        cols = slice(c * chunk, (c + 1) * chunk)
        points = train[:, cols]
        rhs[:dim, cols] = points
        rhs[dim : dim + 16, cols] = norm_rows(half_norms(points), False).astype(BF16)
    get_weight.wait()

    cut = rank // 2
    halves = (pl.ds(0, cut), pl.ds(cut, rank + 8 - cut))

    def place(way, distance):
        return distance if way == 0 or distance in (0, half) else half + distance

    def piece(way, s):
        return halves[(s + way) % 2]

    def hop(axis, way, s):
        rows = piece(way, s)
        return pltpu.make_async_remote_copy(
            src_ref=part.at[axis, place(way, (side - s) // 2), rows],
            dst_ref=recv.at[axis, way, s, pl.ds(0, rows.size)],
            send_sem=s_sem.at[axis, way, s], recv_sem=r_sem.at[axis, way, s],
            device_id={"trn": moved(axis, 1 if way == 0 else -1)},
        )

    def take(axis, way, s, distance):
        hop(axis, way, s).wait_recv()
        rows = piece(way, s)
        at = place(way, distance)
        part[axis, at, rows, :] = part[axis, at, rows, :] + recv[axis, way, s, : rows.size, :]

    def send(axis, s):
        for way in range(2):
            if s >= 2:
                take(axis, way, s - 2, (side - s) // 2)
            hop(axis, way, s).start()

    def compute(starts, axes, places, first):
        points = jnp.concatenate([lhs[pl.ds(s, LANES), :] for s in starts], axis=0)
        total = jnp.zeros((wide, rank), F32)
        weighted = jnp.zeros((wide, LANES), F32)
        for c in range(turns):
            cols = slice(c * chunk, (c + 1) * chunk)
            power = jnp.dot(points, rhs[:, cols], preferred_element_type=F32)
            kern = jnp.exp2(power * F32(8.0 / dim * LOG2E)).astype(BF16)
            if first:
                get_factor[c].wait()
            total = total + jnp.dot(kern, factor[cols, :], preferred_element_type=F32)
            terms = kern.astype(F32) * weight[cols].reshape(1, chunk).astype(F32)
            for g in range(chunk // LANES):
                weighted = weighted + terms[:, g * LANES : (g + 1) * LANES]
        for k in range(2):
            rows = slice(k * LANES, (k + 1) * LANES)
            part[axes[k], places[k], :rank, :] = total[rows].T
            mean_row = jnp.sum(weighted[rows].T, axis=0, keepdims=True)
            part[axes[k], places[k], rank:, :] = jnp.broadcast_to(mean_row, (8, LANES))

    def start_of(axis, distance):
        at = col_pos if isinstance(axis, int) and axis == 0 else row_pos
        if not isinstance(axis, int):
            at = jnp.where(axis == 0, col_pos, row_pos)
        block = lax.rem(at + distance + side, side)
        return pl.multiple_of((block * 2 + axis) * LANES, LANES)

    compute([start_of(0, half), start_of(1, half)], (0, 1), (half, half), True)
    pl.semaphore_wait(barrier, 2 * slots)
    send(0, 0)
    send(1, 0)

    plan = {
        1: [(0, 1)],
        2: [(1, 1)],
        3: [(0, 2), (1, 2)],
        4: [(0, 3), (1, 3)],
        5: [(0, 4), (1, 4)],
        6: [(0, 5), (1, 5), (0, 6), (1, 6)],
    }

    def step(i, carry):
        last = i == slots
        inner = lax.rem(i + 1, 2)
        distance = jnp.where(last, 0, half - lax.div(i + 1, 2))
        axes = (jnp.where(last, 0, inner), jnp.where(last, 1, inner))
        places = (distance, jnp.where(last, 0, half + distance))
        compute([start_of(axes[0], distance), start_of(axes[1], -distance)], axes, places, False)
        for when, sends in plan.items():
            @pl.when(i == when)
            def _(sends=sends):
                for axis, s in sends:
                    send(axis, s)

        return carry

    lax.fori_loop(1, side, step, 0)

    share = rank // side
    order = sorted(range(1, side), key=lambda k: -min(k, side - k))

    def exchange(axis, k):
        peer = lax.rem(pos[1 - axis] + k, side)
        rows = pl.ds(pl.multiple_of(peer * share, share), share)
        return pltpu.make_async_remote_copy(
            src_ref=part.at[axis, 0, rows], dst_ref=share_in.at[axis, k - 1],
            send_sem=ps_sem.at[axis, k - 1], recv_sem=pr_sem.at[axis, k - 1],
            device_id={"trn": moved(1 - axis, k)},
        )

    def add_mean(axis, k):
        return pltpu.make_async_remote_copy(
            src_ref=mean_own.at[axis], dst_ref=mean_in.at[axis, k - 1],
            send_sem=ms_sem, recv_sem=mr_sem, device_id={"trn": moved(1 - axis, k)},
        )

    for axis in range(2):
        for s in (slots - 2, slots - 1):
            for way in range(2):
                take(axis, way, s, 0)
        mean_own[axis] = part[axis, 0, rank : rank + 1, :]
        for k in order:
            exchange(axis, k).start()
            add_mean(axis, k).start()
    for axis in range(2):
        mine = pl.ds(pl.multiple_of(pos[1 - axis] * share, share), share)
        block = part[axis, 0, mine, :]
        for k in order[::-1]:
            exchange(axis, k).wait_recv()
            block = block + share_in[axis, k - 1]
        msg[axis : axis + 1, :] = jnp.sum(block * block, axis=0, keepdims=True)

    far = lambda k: min(k, side - k)
    others = [(kx, ky) for kx in range(side) for ky in range(side) if (kx, ky) != (0, 0)]

    def spread(kx, ky):
        return pltpu.make_async_remote_copy(
            src_ref=msg, dst_ref=gather.at[me], send_sem=gs_sem, recv_sem=gr_sem,
            device_id={"trn": ring[0][kx] + ring[1][ky]},
        )

    for kx, ky in sorted(others, key=lambda k: -far(k[0]) - far(k[1])):
        spread(kx, ky).start()
    gather[me] = msg[...]

    def all_of(ref, send_sem, recv_sem):
        return pltpu.make_async_remote_copy(
            src_ref=ref, dst_ref=ref, send_sem=send_sem, recv_sem=recv_sem, device_id={"trn": moved(0, 1)}
        )

    all_of(mean_in, ms_sem, mr_sem).wait()
    for axis in range(2):
        mean = mean_own[axis]
        for k in range(1, side):
            mean = mean + mean_in[axis, k - 1]
        mean_all[axis, pos[axis]] = mean

    def tell(axis, k):
        return pltpu.make_async_remote_copy(
            src_ref=mean_all.at[axis, pos[axis]], dst_ref=mean_all.at[axis, pos[axis]],
            send_sem=as_sem, recv_sem=ar_sem, device_id={"trn": moved(axis, k)},
        )

    for axis in range(2):
        for k in order:
            tell(axis, k).start()
    for axis in range(2):
        for way in range(2):
            for s in range(slots):
                hop(axis, way, s).wait_send()
        for k in order:
            exchange(axis, k).wait_send()
    all_of(mean_all.at[:, pl.ds(0, slots)], as_sem, ar_sem).wait()
    all_of(gather.at[pl.ds(0, side * side - 1)], gs_sem, gr_sem).wait()
    for p in range(side):
        for axis in range(2):
            total = jnp.zeros((2, LANES), F32)
            for q in range(side):
                total = total + gather[q * side + p if axis == 0 else p * side + q]
            row = 2 * p + axis
            out_ref[0, row : row + 1, :] = total[axis : axis + 1]
            out_ref[1, row : row + 1, :] = -mean_all[axis, p]


def on_device(side, test_points, train_points, weights, factor):
    dim, rows = test_points.shape
    local, rank = factor.shape
    slots = side - 1
    share = rank // side
    chunk = 1024
    dma = pltpu.SemaphoreType.DMA
    out = pl.pallas_call(
        functools.partial(body, side, chunk),
        out_shape=jax.ShapeDtypeStruct((2, rows // LANES, LANES), F32),
        in_specs=[pl.BlockSpec(memory_space=pl.ANY)] * 4,
        out_specs=pl.BlockSpec(memory_space=pltpu.VMEM),
        scratch_shapes=[
            pltpu.VMEM((dim, rows), BF16),
            pltpu.VMEM((dim, local), BF16),
            pltpu.VMEM((local,), BF16),
            pltpu.VMEM((local, rank), BF16),
            pltpu.VMEM((rows, LANES), BF16),
            pltpu.VMEM((LANES, local), BF16),
            pltpu.VMEM((2, side, rank + 8, LANES), F32),
            pltpu.VMEM((2, 2, slots, rank // 2 + 8, LANES), F32),
            pltpu.VMEM((2, slots, share, LANES), F32),
            pltpu.VMEM((2, 1, LANES), F32),
            pltpu.VMEM((2, slots, 1, LANES), F32),
            pltpu.VMEM((2, side, 1, LANES), F32),
            pltpu.VMEM((2, LANES), F32),
            pltpu.VMEM((side * side, 2, LANES), F32),
            dma((3 + local // chunk,)),
            dma((2, 2, slots)), dma((2, 2, slots)),
            dma((2, slots)), dma((2, slots)),
            dma, dma, dma, dma, dma, dma,
        ],
        compiler_params=pltpu.CompilerParams(
            collective_id=0, has_side_effects=True, vmem_limit_bytes=56 * 1024 * 1024
        ),
    )(test_points, train_points, weights, factor)
    return -out[1].reshape(rows), 1.0 - out[0].reshape(rows)


def solution(mesh):
    side = math.isqrt(mesh.shape["trn"])
    shared = ("grp", "trn")
    return jax.shard_map(
        functools.partial(on_device, side),
        mesh=mesh,
        in_specs=(P(None, ("grp", "tst")), P(None, shared), P(shared), P(shared, None)),
        out_specs=(P(("grp", "tst")), P(("grp", "tst"))),
        check_vma=False,
    )
```

time: 64.9 us -> 61.3 us (0.945)
  Pallas kernels: 62.7 us -> 59.1 us
    pallas_call x1, Pallas kernels: 62.7 us -> 59.1 us  [on_device(): pl.pallas_call(functools.partial(body, side, chunk), out_shape=jax.ShapeD...]
where the time goes in v3:
time: 61.3 us; the launch traced here: 61.1 us
  Pallas kernels  59.1 us (96%)
  other arithmetic  1.32 us (2%)
  between operations  0.64 us (1%)
    pallas_call x1, Pallas kernels, on_device(): pl.pallas_call(functools.partial(body, side, chunk), out_shape=jax.ShapeD...  59.1 us
    sub x1, other arithmetic, on_device(): return (-out[1].reshape(rows), 1.0 - out[0].reshape(rows))  1.32 us

profile of v3, /device:TPU:514, one launch (start us, length us, event | category | flops | bytes accessed | tf_op | source)
XLA Modules:
  0.0 61.1 jit_solution(2356819469008099461)
XLA Ops:
  0.6 59.1 %shard_map.59 = f32[2,16,128]{2,1,0:T(8,128)} custom-call(bf16[64,2048]{1,0:T(8,128)(2,1)} %test_hbm.1, bf16[64,4096]{1,0:T(8,128)(2,1)} %train_hbm.1, bf16[4096]{0:T(1024)(128)(2,1)} %weight_hbm.1, bf16[4096,512]{1,0:T(8,128)(2,1)} %factor_hbm.1), custom_call_target="tpu_custom_call" | custom-call | tf_op jit(solution)/shard_map/pallas_call | solution.py:277
  59.8 1.3 %subtract_bitcast_fusion = (f32[2048]{0:T(1024)}, f32[2048]{0:T(1024)}) fusion(f32[2,16,128]{2,1,0:T(8,128)} %shard_map.59), kind=kLoop, calls=%fused_computation | loop fusion | flops 4096 | bytes 32768 | tf_op jit(solution)/shard_map/sub | solution.py:306

commit v4 on v3

--- a/solution.py
+++ b/solution.py
@@ -68,75 +68,81 @@
     get_test = load(0, test_hbm, test)
     get_train = load(1, train_hbm, train)
     get_weight = load(2, weight_hbm, weight)
+    barrier = pltpu.get_barrier_semaphore()
+    for axis in range(2):
+        for k in (1, -1):
+            pl.semaphore_signal(barrier, inc=1, device_id={"trn": moved(axis, k)})
+
+    pad = jnp.zeros((LANES - dim - 16, LANES), F32)
+    get_test.wait()
     get_factor = []
     for c in range(turns):
         rows = pl.ds(c * chunk, chunk)
         get_factor.append(load(3 + c, factor_hbm.at[rows], factor.at[rows]))
-    barrier = pltpu.get_barrier_semaphore()
-    for axis in range(2):
-        for k in range(1, side):
-            pl.semaphore_signal(barrier, inc=1, device_id={"trn": moved(axis, k)})
-
-    pad = jnp.zeros((LANES - dim - 16, LANES), F32)
-    get_test.wait()
     for b in range(test.shape[1] // LANES):
         cols = slice(b * LANES, (b + 1) * LANES)
         points = test[:, cols].astype(F32)
         stack = jnp.concatenate([points, norm_rows(half_norms(points), True), pad], axis=0)
         lhs[cols, :] = stack.T.astype(BF16)
     get_train.wait()
-    rhs[dim + 16 :, :] = jnp.zeros((LANES - dim - 16, local), BF16)
-    for c in range(turns):
-        cols = slice(c * chunk, (c + 1) * chunk)
-        points = train[:, cols]
-        rhs[:dim, cols] = points
-        rhs[dim : dim + 16, cols] = norm_rows(half_norms(points), False).astype(BF16)
     get_weight.wait()
 
-    cut = rank // 2
-    halves = (pl.ds(0, cut), pl.ds(cut, rank + 8 - cut))
+    quarter = rank // 4
+    ends = [quarter * g for g in range(4)] + [rank + 1]
+    quarters = [pl.ds(ends[g], ends[g + 1] - ends[g]) for g in range(4)]
 
     def place(way, distance):
         return distance if way == 0 or distance in (0, half) else half + distance
 
-    def piece(way, s):
-        return halves[(s + way) % 2]
-
-    def hop(axis, way, s):
-        rows = piece(way, s)
+    def piece(way, s, j):
+        return quarters[2 * ((s + way) % 2) + j]
+
+    def hop(axis, way, s, j):
+        rows = piece(way, s, j)
         return pltpu.make_async_remote_copy(
             src_ref=part.at[axis, place(way, (side - s) // 2), rows],
-            dst_ref=recv.at[axis, way, s, pl.ds(0, rows.size)],
-            send_sem=s_sem.at[axis, way, s], recv_sem=r_sem.at[axis, way, s],
+            dst_ref=recv.at[axis, way, s, j, pl.ds(0, rows.size)],
+            send_sem=s_sem.at[axis, way, s, j], recv_sem=r_sem.at[axis, way, s, j],
             device_id={"trn": moved(axis, 1 if way == 0 else -1)},
         )
 
-    def take(axis, way, s, distance):
-        hop(axis, way, s).wait_recv()
-        rows = piece(way, s)
+    def take(axis, way, s, distance, j):
+        hop(axis, way, s, j).wait_recv()
+        rows = piece(way, s, j)
         at = place(way, distance)
-        part[axis, at, rows, :] = part[axis, at, rows, :] + recv[axis, way, s, : rows.size, :]
-
-    def send(axis, s):
-        for way in range(2):
-            if s >= 2:
-                take(axis, way, s - 2, (side - s) // 2)
-            hop(axis, way, s).start()
+        part[axis, at, rows, :] = part[axis, at, rows, :] + recv[axis, way, s, j, : rows.size, :]
+
+    def send(sends):
+        for j in range(2):
+            for axis, s in sends:
+                for way in range(2):
+                    if s >= 2:
+                        take(axis, way, s - 2, (side - s) // 2, j)
+                    hop(axis, way, s, j).start()
 
     def compute(starts, axes, places, first):
         points = jnp.concatenate([lhs[pl.ds(s, LANES), :] for s in starts], axis=0)
         total = jnp.zeros((wide, rank), F32)
         weighted = jnp.zeros((wide, LANES), F32)
+        kerns = []
         for c in range(turns):
             cols = slice(c * chunk, (c + 1) * chunk)
+            if first:
+                rhs[:dim, cols] = train[:, cols]
+                rhs[dim : dim + 16, cols] = norm_rows(half_norms(train[:, cols]), False).astype(BF16)
+                rhs[dim + 16 :, cols] = jnp.zeros((LANES - dim - 16, chunk), BF16)
             power = jnp.dot(points, rhs[:, cols], preferred_element_type=F32)
             kern = jnp.exp2(power * F32(8.0 / dim * LOG2E)).astype(BF16)
-            if first:
-                get_factor[c].wait()
-            total = total + jnp.dot(kern, factor[cols, :], preferred_element_type=F32)
             terms = kern.astype(F32) * weight[cols].reshape(1, chunk).astype(F32)
             for g in range(chunk // LANES):
                 weighted = weighted + terms[:, g * LANES : (g + 1) * LANES]
+            if first:
+                kerns.append(kern)
+            else:
+                total = total + jnp.dot(kern, factor[cols, :], preferred_element_type=F32)
+        for c, kern in enumerate(kerns):
+            get_factor[c].wait()
+            total = total + jnp.dot(kern, factor[c * chunk : (c + 1) * chunk, :], preferred_element_type=F32)
         for k in range(2):
             rows = slice(k * LANES, (k + 1) * LANES)
             part[axes[k], places[k], :rank, :] = total[rows].T
@@ -151,18 +157,28 @@
         return pl.multiple_of((block * 2 + axis) * LANES, LANES)
 
     compute([start_of(0, half), start_of(1, half)], (0, 1), (half, half), True)
-    pl.semaphore_wait(barrier, 2 * slots)
-    send(0, 0)
-    send(1, 0)
-
-    plan = {
-        1: [(0, 1)],
-        2: [(1, 1)],
-        3: [(0, 2), (1, 2)],
-        4: [(0, 3), (1, 3)],
-        5: [(0, 4), (1, 4)],
-        6: [(0, 5), (1, 5), (0, 6), (1, 6)],
-    }
+    pl.semaphore_wait(barrier, 4)
+    plan = [
+        (0, [(0, 0), (1, 0)]),
+        (1, [(0, 1)]),
+        (2, [(1, 1)]),
+        (3, [(0, 2), (1, 2)]),
+        (4, [(0, 3), (1, 3)]),
+        (5, [(0, 4), (1, 4)]),
+        (6, [(0, 5), (1, 5)]),
+        (6, [(0, 6), (1, 6)]),
+    ]
+
+    def events(i):
+        for when, sends in plan:
+            if when == 0:
+                continue
+
+            @pl.when(i == when)
+            def _(sends=sends):
+                send(sends)
+
+    send(plan[0][1])
 
     def step(i, carry):
         last = i == slots
@@ -171,25 +187,20 @@
         axes = (jnp.where(last, 0, inner), jnp.where(last, 1, inner))
         places = (distance, jnp.where(last, 0, half + distance))
         compute([start_of(axes[0], distance), start_of(axes[1], -distance)], axes, places, False)
-        for when, sends in plan.items():
-            @pl.when(i == when)
-            def _(sends=sends):
-                for axis, s in sends:
-                    send(axis, s)
-
+        events(i)
         return carry
 
     lax.fori_loop(1, side, step, 0)
 
-    share = rank // side
+    share = quarter // side
     order = sorted(range(1, side), key=lambda k: -min(k, side - k))
 
-    def exchange(axis, k):
+    def exchange(axis, g, k):
         peer = lax.rem(pos[1 - axis] + k, side)
-        rows = pl.ds(pl.multiple_of(peer * share, share), share)
-        return pltpu.make_async_remote_copy(
-            src_ref=part.at[axis, 0, rows], dst_ref=share_in.at[axis, k - 1],
-            send_sem=ps_sem.at[axis, k - 1], recv_sem=pr_sem.at[axis, k - 1],
+        rows = pl.ds(pl.multiple_of(quarter * g + peer * share, share), share)
+        return pltpu.make_async_remote_copy(
+            src_ref=part.at[axis, 0, rows], dst_ref=share_in.at[axis, g, k - 1],
+            send_sem=ps_sem.at[axis, g], recv_sem=pr_sem.at[axis, g],
             device_id={"trn": moved(1 - axis, k)},
         )
 
@@ -199,21 +210,34 @@
             send_sem=ms_sem, recv_sem=mr_sem, device_id={"trn": moved(1 - axis, k)},
         )
 
-    for axis in range(2):
-        for s in (slots - 2, slots - 1):
+    def all_of(ref, send_sem, recv_sem):
+        return pltpu.make_async_remote_copy(
+            src_ref=ref, dst_ref=ref, send_sem=send_sem, recv_sem=recv_sem, device_id={"trn": moved(0, 1)}
+        )
+
+    for j in range(2):
+        for axis in range(2):
             for way in range(2):
-                take(axis, way, s, 0)
+                take(axis, way, slots - 2, 0, j)
+    for j in range(2):
+        for axis in range(2):
+            for way in range(2):
+                take(axis, way, slots - 1, 0, j)
+                for k in order:
+                    exchange(axis, 2 * ((slots - 1 + way) % 2) + j, k).start()
+    for axis in range(2):
         mean_own[axis] = part[axis, 0, rank : rank + 1, :]
         for k in order:
-            exchange(axis, k).start()
             add_mean(axis, k).start()
     for axis in range(2):
-        mine = pl.ds(pl.multiple_of(pos[1 - axis] * share, share), share)
-        block = part[axis, 0, mine, :]
-        for k in order[::-1]:
-            exchange(axis, k).wait_recv()
-            block = block + share_in[axis, k - 1]
-        msg[axis : axis + 1, :] = jnp.sum(block * block, axis=0, keepdims=True)
+        total = jnp.zeros((1, LANES), F32)
+        for g in (0, 2, 1, 3):
+            all_of(share_in.at[axis, g], ps_sem.at[axis, g], pr_sem.at[axis, g]).wait_recv()
+            block = part[axis, 0, pl.ds(pl.multiple_of(quarter * g + pos[1 - axis] * share, share), share), :]
+            for k in range(slots):
+                block = block + share_in[axis, g, k]
+            total = total + jnp.sum(block * block, axis=0, keepdims=True)
+        msg[axis : axis + 1, :] = total
 
     far = lambda k: min(k, side - k)
     others = [(kx, ky) for kx in range(side) for ky in range(side) if (kx, ky) != (0, 0)]
@@ -227,11 +251,6 @@
     for kx, ky in sorted(others, key=lambda k: -far(k[0]) - far(k[1])):
         spread(kx, ky).start()
     gather[me] = msg[...]
-
-    def all_of(ref, send_sem, recv_sem):
-        return pltpu.make_async_remote_copy(
-            src_ref=ref, dst_ref=ref, send_sem=send_sem, recv_sem=recv_sem, device_id={"trn": moved(0, 1)}
-        )
 
     all_of(mean_in, ms_sem, mr_sem).wait()
     for axis in range(2):
@@ -252,9 +271,10 @@
     for axis in range(2):
         for way in range(2):
             for s in range(slots):
-                hop(axis, way, s).wait_send()
-        for k in order:
-            exchange(axis, k).wait_send()
+                for j in range(2):
+                    hop(axis, way, s, j).wait_send()
+        for g in range(4):
+            all_of(share_in.at[axis, g], ps_sem.at[axis, g], pr_sem.at[axis, g]).wait_send()
     all_of(mean_all.at[:, pl.ds(0, slots)], as_sem, ar_sem).wait()
     all_of(gather.at[pl.ds(0, side * side - 1)], gs_sem, gr_sem).wait()
     for p in range(side):
@@ -271,7 +291,7 @@
     dim, rows = test_points.shape
     local, rank = factor.shape
     slots = side - 1
-    share = rank // side
+    share = rank // 4 // side
     chunk = 1024
     dma = pltpu.SemaphoreType.DMA
     out = pl.pallas_call(
@@ -287,22 +307,22 @@
             pltpu.VMEM((rows, LANES), BF16),
             pltpu.VMEM((LANES, local), BF16),
             pltpu.VMEM((2, side, rank + 8, LANES), F32),
-            pltpu.VMEM((2, 2, slots, rank // 2 + 8, LANES), F32),
-            pltpu.VMEM((2, slots, share, LANES), F32),
+            pltpu.VMEM((2, 2, slots, 2, rank // 4 + 8, LANES), F32),
+            pltpu.VMEM((2, 4, slots, share, LANES), F32),
             pltpu.VMEM((2, 1, LANES), F32),
             pltpu.VMEM((2, slots, 1, LANES), F32),
             pltpu.VMEM((2, side, 1, LANES), F32),
             pltpu.VMEM((2, LANES), F32),
             pltpu.VMEM((side * side, 2, LANES), F32),
             dma((3 + local // chunk,)),
-            dma((2, 2, slots)), dma((2, 2, slots)),
-            dma((2, slots)), dma((2, slots)),
+            dma((2, 2, slots, 2)), dma((2, 2, slots, 2)),
+            dma((2, 4)), dma((2, 4)),
             dma, dma, dma, dma, dma, dma,
         ],
         compiler_params=pltpu.CompilerParams(
-            collective_id=0, has_side_effects=True, vmem_limit_bytes=56 * 1024 * 1024
+            collective_id=0, has_side_effects=True, vmem_limit_bytes=40 * 1024 * 1024
         ),
-    )(test_points, train_points, weights, factor)
+    )(*(pltpu.with_memory_space_constraint(x, pltpu.HBM) for x in (test_points, train_points, weights, factor)))
     return -out[1].reshape(rows), 1.0 - out[0].reshape(rows)
 
 

time: 61.3 us -> 59.1 us (0.964)
  Pallas kernels: 59.1 us -> 57.8 us
  other arithmetic: 1.32 us -> 0.61 us
    pallas_call x1, Pallas kernels: 59.1 us -> 57.8 us  [on_device(): pl.pallas_call(functools.partial(body, side, chunk), out_shape=jax.ShapeD...]
    sub x1, other arithmetic: 1.32 us -> 0.61 us  [on_device(): return (-out[1].reshape(rows), 1.0 - out[0].reshape(rows))]
where the time goes in v4:
time: 59.1 us; the launch traced here: 59 us
  Pallas kernels  57.8 us (98%)
  between operations  0.64 us (1%)
  other arithmetic  0.61 us (1%)
    pallas_call x1, Pallas kernels, on_device(): pl.pallas_call(functools.partial(body, side, chunk), out_shape=jax.ShapeD...  57.8 us

profile of v4, /device:TPU:514, one launch (start us, length us, event | category | flops | bytes accessed | tf_op | source)
XLA Modules:
  0.0 59.0 jit_solution(764404726337162424)
XLA Ops:
  0.6 57.8 %shard_map.59 = f32[2,16,128]{2,1,0:T(8,128)S(1)} custom-call(bf16[64,2048]{1,0:T(8,128)(2,1)} %test_hbm.1, bf16[64,4096]{1,0:T(8,128)(2,1)} %train_hbm.1, bf16[4096]{0:T(1024)(128)(2,1)} %weight_hbm.1, bf16[4096,512]{1,0:T(8,128)(2,1)} %factor_hbm.1), custom_call_target="tpu_custom_call" | custom-call | tf_op jit(solution)/shard_map/pallas_call | solution.py:297
  58.4 0.6 %subtract_bitcast_fusion = (f32[2048]{0:T(1024)}, f32[2048]{0:T(1024)}) fusion(f32[2,16,128]{2,1,0:T(8,128)S(1)} %shard_map.59), kind=kLoop, calls=%fused_computation | loop fusion | flops 4096 | bytes 32768 | tf_op jit(solution)/shard_map/sub | solution.py:326

commit v5 on v4

--- a/solution.py
+++ b/solution.py
@@ -68,6 +68,12 @@
     get_test = load(0, test_hbm, test)
     get_train = load(1, train_hbm, train)
     get_weight = load(2, weight_hbm, weight)
+
+    def load_factor(c):
+        rows = pl.ds(c * chunk, chunk)
+        return load(3 + c, factor_hbm.at[rows], factor.at[rows])
+
+    get_factor = [load_factor(0)]
     barrier = pltpu.get_barrier_semaphore()
     for axis in range(2):
         for k in (1, -1):
@@ -75,10 +81,7 @@
 
     pad = jnp.zeros((LANES - dim - 16, LANES), F32)
     get_test.wait()
-    get_factor = []
-    for c in range(turns):
-        rows = pl.ds(c * chunk, chunk)
-        get_factor.append(load(3 + c, factor_hbm.at[rows], factor.at[rows]))
+    get_factor += [load_factor(c) for c in range(1, turns)]
     for b in range(test.shape[1] // LANES):
         cols = slice(b * LANES, (b + 1) * LANES)
         points = test[:, cols].astype(F32)

time: 59.1 us -> 58.8 us (level)
  no operation moved by 1% of the time
where the time goes in v5:
time: 58.8 us; the launch traced here: 58.7 us
  Pallas kernels  57.4 us (98%)
  between operations  0.64 us (1%)
  other arithmetic  0.61 us (1%)
    pallas_call x1, Pallas kernels, on_device(): pl.pallas_call(functools.partial(body, side, chunk), out_shape=jax.ShapeD...  57.4 us

profile of v5, /device:TPU:514, one launch (start us, length us, event | category | flops | bytes accessed | tf_op | source)
XLA Modules:
  0.0 58.7 jit_solution(1623392363518702314)
XLA Ops:
  0.6 57.4 %shard_map.59 = f32[2,16,128]{2,1,0:T(8,128)S(1)} custom-call(bf16[64,2048]{1,0:T(8,128)(2,1)} %test_hbm.1, bf16[64,4096]{1,0:T(8,128)(2,1)} %train_hbm.1, bf16[4096]{0:T(1024)(128)(2,1)} %weight_hbm.1, bf16[4096,512]{1,0:T(8,128)(2,1)} %factor_hbm.1), custom_call_target="tpu_custom_call" | custom-call | tf_op jit(solution)/shard_map/pallas_call | solution.py:300
  58.1 0.6 %subtract_bitcast_fusion = (f32[2048]{0:T(1024)}, f32[2048]{0:T(1024)}) fusion(f32[2,16,128]{2,1,0:T(8,128)S(1)} %shard_map.59), kind=kLoop, calls=%fused_computation | loop fusion | flops 4096 | bytes 32768 | tf_op jit(solution)/shard_map/sub | solution.py:329

commit v6 on v5

--- a/solution.py
+++ b/solution.py
@@ -90,15 +90,15 @@
     get_train.wait()
     get_weight.wait()
 
-    quarter = rank // 4
-    ends = [quarter * g for g in range(4)] + [rank + 1]
-    quarters = [pl.ds(ends[g], ends[g + 1] - ends[g]) for g in range(4)]
+    quarter = rank // 2
+    ends = [quarter * g for g in range(2)] + [rank + 1]
+    quarters = [pl.ds(ends[g], ends[g + 1] - ends[g]) for g in range(2)]
 
     def place(way, distance):
         return distance if way == 0 or distance in (0, half) else half + distance
 
     def piece(way, s, j):
-        return quarters[2 * ((s + way) % 2) + j]
+        return quarters[(s + way) % 2 + j]
 
     def hop(axis, way, s, j):
         rows = piece(way, s, j)
@@ -116,7 +116,7 @@
         part[axis, at, rows, :] = part[axis, at, rows, :] + recv[axis, way, s, j, : rows.size, :]
 
     def send(sends):
-        for j in range(2):
+        for j in range(1):
             for axis, s in sends:
                 for way in range(2):
                     if s >= 2:
@@ -165,7 +165,7 @@
         (0, [(0, 0), (1, 0)]),
         (1, [(0, 1)]),
         (2, [(1, 1)]),
-        (3, [(0, 2), (1, 2)]),
+        (2, [(0, 2), (1, 2)]),
         (4, [(0, 3), (1, 3)]),
         (5, [(0, 4), (1, 4)]),
         (6, [(0, 5), (1, 5)]),
@@ -218,23 +218,23 @@
             src_ref=ref, dst_ref=ref, send_sem=send_sem, recv_sem=recv_sem, device_id={"trn": moved(0, 1)}
         )
 
-    for j in range(2):
+    for j in range(1):
         for axis in range(2):
             for way in range(2):
                 take(axis, way, slots - 2, 0, j)
-    for j in range(2):
+    for j in range(1):
         for axis in range(2):
             for way in range(2):
                 take(axis, way, slots - 1, 0, j)
                 for k in order:
-                    exchange(axis, 2 * ((slots - 1 + way) % 2) + j, k).start()
+                    exchange(axis, (slots - 1 + way) % 2 + j, k).start()
     for axis in range(2):
         mean_own[axis] = part[axis, 0, rank : rank + 1, :]
         for k in order:
             add_mean(axis, k).start()
     for axis in range(2):
         total = jnp.zeros((1, LANES), F32)
-        for g in (0, 2, 1, 3):
+        for g in (0, 1):
             all_of(share_in.at[axis, g], ps_sem.at[axis, g], pr_sem.at[axis, g]).wait_recv()
             block = part[axis, 0, pl.ds(pl.multiple_of(quarter * g + pos[1 - axis] * share, share), share), :]
             for k in range(slots):
@@ -274,9 +274,9 @@
     for axis in range(2):
         for way in range(2):
             for s in range(slots):
-                for j in range(2):
+                for j in range(1):
                     hop(axis, way, s, j).wait_send()
-        for g in range(4):
+        for g in range(2):
             all_of(share_in.at[axis, g], ps_sem.at[axis, g], pr_sem.at[axis, g]).wait_send()
     all_of(mean_all.at[:, pl.ds(0, slots)], as_sem, ar_sem).wait()
     all_of(gather.at[pl.ds(0, side * side - 1)], gs_sem, gr_sem).wait()
@@ -294,7 +294,7 @@
     dim, rows = test_points.shape
     local, rank = factor.shape
     slots = side - 1
-    share = rank // 4 // side
+    share = rank // 2 // side
     chunk = 1024
     dma = pltpu.SemaphoreType.DMA
     out = pl.pallas_call(
@@ -310,16 +310,16 @@
             pltpu.VMEM((rows, LANES), BF16),
             pltpu.VMEM((LANES, local), BF16),
             pltpu.VMEM((2, side, rank + 8, LANES), F32),
-            pltpu.VMEM((2, 2, slots, 2, rank // 4 + 8, LANES), F32),
-            pltpu.VMEM((2, 4, slots, share, LANES), F32),
+            pltpu.VMEM((2, 2, slots, 1, rank // 2 + 8, LANES), F32),
+            pltpu.VMEM((2, 2, slots, share, LANES), F32),
             pltpu.VMEM((2, 1, LANES), F32),
             pltpu.VMEM((2, slots, 1, LANES), F32),
             pltpu.VMEM((2, side, 1, LANES), F32),
             pltpu.VMEM((2, LANES), F32),
             pltpu.VMEM((side * side, 2, LANES), F32),
             dma((3 + local // chunk,)),
-            dma((2, 2, slots, 2)), dma((2, 2, slots, 2)),
-            dma((2, 4)), dma((2, 4)),
+            dma((2, 2, slots, 1)), dma((2, 2, slots, 1)),
+            dma((2, 2)), dma((2, 2)),
             dma, dma, dma, dma, dma, dma,
         ],
         compiler_params=pltpu.CompilerParams(

time: 58.8 us -> 59.5 us (1.012)
  Pallas kernels: 57.4 us -> 58.1 us
    pallas_call x1, Pallas kernels: 57.4 us -> 58.1 us  [on_device(): pl.pallas_call(functools.partial(body, side, chunk), out_shape=jax.ShapeD...]
where the time goes in v6:
time: 59.5 us; the launch traced here: 59.3 us
  Pallas kernels  58.1 us (98%)
  between operations  0.64 us (1%)
  other arithmetic  0.61 us (1%)
    pallas_call x1, Pallas kernels, on_device(): pl.pallas_call(functools.partial(body, side, chunk), out_shape=jax.ShapeD...  58.1 us

profile of v6, /device:TPU:514, one launch (start us, length us, event | category | flops | bytes accessed | tf_op | source)
XLA Modules:
  0.0 59.3 jit_solution(10376503122852263799)
XLA Ops:
  0.6 58.1 %shard_map.59 = f32[2,16,128]{2,1,0:T(8,128)S(1)} custom-call(bf16[64,2048]{1,0:T(8,128)(2,1)} %test_hbm.1, bf16[64,4096]{1,0:T(8,128)(2,1)} %train_hbm.1, bf16[4096]{0:T(1024)(128)(2,1)} %weight_hbm.1, bf16[4096,512]{1,0:T(8,128)(2,1)} %factor_hbm.1), custom_call_target="tpu_custom_call" | custom-call | tf_op jit(solution)/shard_map/pallas_call | solution.py:300
  58.7 0.6 %subtract_bitcast_fusion = (f32[2048]{0:T(1024)}, f32[2048]{0:T(1024)}) fusion(f32[2,16,128]{2,1,0:T(8,128)S(1)} %shard_map.59), kind=kLoop, calls=%fused_computation | loop fusion | flops 4096 | bytes 32768 | tf_op jit(solution)/shard_map/sub | solution.py:329
